TPU v7x, 32 devices: a whole 2x2x4 slice. The times are simulated.
32 devices in a mesh: layer: 2 (over core), row: 4 (over y, x), col: 4 (over z).
Axes of the slice: x: 2, y: 2, z: 4, core: 2. Of those that a mesh axis runs over, the one named last changes fastest.
Arguments:
- root_rhs: float32 [32, 8, 1024], P(None, None, 'row'), may hold values from -6 to 6
- child_rhs: float32 [2, 32, 8, 1024], P('layer', None, None, 'row'), may hold values from -6 to 6
- root_factor: float32 [8, 8, 1024, 1024], P(None, None, 'row', 'col'), may hold values from -0.0625 to 0.0625
- child_factor: float32 [2, 8, 8, 1024, 1024], P('layer', None, None, 'row', 'col'), may hold values from -0.0625 to 0.0625
- coupling: float32 [2, 8, 8, 1024, 1024], P('layer', None, None, 'row', 'col'), may hold values from -0.0234375 to 0.0234375
- root_inverse: float32 [8, 1024, 1024], P(None, 'col', 'row'), as said below
- child_inverse: float32 [2, 8, 1024, 1024], P('layer', None, 'col', 'row'), as said below
Outputs:
- root_solution: float32 [32, 8, 1024], P(None, None, 'row')
- child_solution: float32 [2, 32, 8, 1024], P('layer', None, None, 'row')
Inputs may be any that keep to these rules, and one draw needn't show every extreme that they name: Each block of root_inverse is lower triangular. Each block of child_inverse is lower triangular.
All inputs are finite; a program needn't handle non-finite values.
Results may differ from a plain program's by a relative error of at most 0.00015.
Values sent between devices are 32-bit elements; how exact they have to be, the bound alone decides.
No kernel may reach another device: no remote copies, remote signals or barrier semaphores. Data moves between devices by JAX's collectives and lax.ppermute only.
A program may use at most 128 MiB of HBM per device.

v0:
```python
import jax
import jax.numpy as jnp
from jax import lax
from jax.sharding import PartitionSpec as P

precise = lax.Precision.HIGHEST


def pick(stack, index, axis):
    return lax.dynamic_index_in_dim(stack, index, axis, keepdims=False)


def forward(factor, inverse, right, extra, first_col):
    blocks = factor.shape[0]
    columns = right.shape[0]
    col_width = factor.shape[3]
    right_rows = jnp.transpose(right, (1, 0, 2))
    solved = jnp.zeros((blocks, columns, col_width), jnp.float32)

    def forward_step(target, solved):
        row_tiles = pick(factor, target, 0)
        partial_value = jnp.where(first_col, pick(right_rows, target, 0), 0.0) - pick(
            extra, target, 0
        )
        partial_value = partial_value - jnp.einsum(
            "jna,jba->nb", solved, row_tiles, precision=precise
        )
        residual = lax.psum(partial_value, "col")
        share = jnp.einsum("nb,ab->na", residual, pick(inverse, target, 0), precision=precise)
        solved_block = lax.psum(share, "row")
        return lax.dynamic_update_index_in_dim(solved, solved_block, target, 0)

    return lax.fori_loop(0, blocks, forward_step, solved)


def backward(factor, inverse, values, lowered, first_row):
    blocks = factor.shape[0]
    columns = values.shape[1]
    row_width = factor.shape[2]
    solved = jnp.zeros((blocks, columns, row_width), jnp.float32)

    def backward_step(step_at, solved):
        target = blocks - 1 - step_at
        column_tiles = pick(factor, target, 1)
        partial_value = jnp.where(first_row, pick(values, target, 0), 0.0) - pick(
            lowered, target, 0
        )
        partial_value = partial_value - jnp.einsum(
            "inb,iba->na", solved, column_tiles, precision=precise
        )
        pending = lax.psum(partial_value, "row")
        share = jnp.einsum("na,ab->nb", pending, pick(inverse, target, 0), precision=precise)
        solved_block = lax.psum(share, "col")
        return lax.dynamic_update_index_in_dim(solved, solved_block, target, 0)

    return lax.fori_loop(0, blocks, backward_step, solved)


def local(root_rhs, child_rhs, root_factor, child_factor, coupling, root_inverse, child_inverse):
    first_row = lax.axis_index("row") == 0
    first_col = lax.axis_index("col") == 0
    columns = root_rhs.shape[0]
    child_blocks = child_factor[0]
    child_inverses = child_inverse[0]
    couple_blocks = coupling[0]
    child_count = child_blocks.shape[0]
    root_count = root_factor.shape[0]
    row_width = root_factor.shape[2]
    col_width = root_factor.shape[3]
    child_down, root_down = (child_inverses, root_inverse)
    child_up, root_up = (child_inverses, root_inverse)
    child_start = jnp.zeros((child_count, columns, row_width), jnp.float32)
    child_forward = forward(child_blocks, child_down, child_rhs[0], child_start, first_col)
    lifted = jnp.einsum("jna,kjba->knb", child_forward, couple_blocks, precision=precise)
    lifted = lax.psum_scatter(lifted, "layer", scatter_dimension=1, tiled=True)
    half_cols = lifted.shape[1]
    layer_index = lax.axis_index("layer")
    right_half = lax.dynamic_slice_in_dim(root_rhs, layer_index * half_cols, half_cols, 0)
    root_forward = forward(root_factor, root_down, right_half, lifted, first_col)
    empty = jnp.zeros((root_count, half_cols, col_width), jnp.float32)
    root_half = backward(root_factor, root_up, root_forward, empty, first_row)
    root_solved = lax.all_gather(root_half, "layer", axis=1, tiled=True)
    lowered = jnp.einsum("inb,ikba->kna", root_solved, couple_blocks, precision=precise)
    child_solved = backward(child_blocks, child_up, child_forward, lowered, first_row)
    root_solution = jnp.transpose(root_solved, (1, 0, 2))
    child_solution = jnp.transpose(child_solved, (1, 0, 2))[None]
    return (root_solution, child_solution)


def solution(mesh):
    in_specs = (
        P(None, None, "row"),
        P("layer", None, None, "row"),
        P(None, None, "row", "col"),
        P("layer", None, None, "row", "col"),
        P("layer", None, None, "row", "col"),
        P(None, "col", "row"),
        P("layer", None, "col", "row"),
    )
    out_specs = (P(None, None, "row"), P("layer", None, None, "row"))
    return jax.shard_map(local, mesh=mesh, in_specs=in_specs, out_specs=out_specs, check_vma=False)
```

profile of v0, /device:TPU:0, one launch (start us, length us, event | category | flops | bytes accessed | tf_op | source)
XLA Modules:
  0.0 1199.0 jit_solution(10742382642102309621)
XLA Ops:
  8.3 295.6 %while.56 = (s32[]{:T(128)}, f32[8,32,256]{2,1,0:T(8,128)S(1)}, pred[]{:T(512)}, f32[8,32,256]{2,1,0:T(8,128)S(1)}, f32[8,8,256,256]{3,2,1,0:T(8,128)}, /*index=5*/f32[8,256,256]{2,1,0:T(8,128)}, s32[]{:T(128)}) while((s32[]{:T(128)}, f32[8,32,256]{2,1,0:T(8,128)S(1)}, pred[]{:T(512)}, f32[8,32,256]{2,1,0:T(8,128)S(1)}, ...), condition=%wide.region_3.4_spmd, body=%wide.region_0.3_spmd.sunk | while | flops 226525184 | bytes 2950749 | solution.py:33
  11.8 20.9 %psum.108 = f32[32,256]{1,0:T(8,128)S(1)} all-reduce(f32[32,256]{1,0:T(8,128)S(1)} %fusion.96), channel_id=1, replica_groups=mesh['layer'=2,'row'=4,'col'=4] {'col'}, use_global_device_ids=true, to_apply=%region_1.1 | all-reduce | flops 8192 | bytes 65536 | tf_op jit(solution)/shard_map/while/body/eval_jaxpr/psum | solution.py:28
  34.0 16.3 %psum.109 = f32[1,32,256]{2,1,0:T(8,128)S(1)} all-reduce(f32[1,32,256]{2,1,0:T(8,128)S(1)} %convolution_bitcast_fusion.8), channel_id=1, replica_groups=mesh['layer'=2,'row'=4,'col'=4] {'row'}, use_global_device_ids=true, to_apply=%region_2.2 | all-reduce | flops 8192 | bytes 65536 | tf_op jit(solution)/shard_map/while/body/eval_jaxpr/psum | solution.py:30
  53.8 15.8 %psum.108 = f32[32,256]{1,0:T(8,128)S(1)} all-reduce(f32[32,256]{1,0:T(8,128)S(1)} %fusion.96), channel_id=1, replica_groups=mesh['layer'=2,'row'=4,'col'=4] {'col'}, use_global_device_ids=true, to_apply=%region_1.1 | all-reduce | flops 8192 | bytes 65536 | tf_op jit(solution)/shard_map/while/body/eval_jaxpr/psum | solution.py:28
  88.6 17.5 %psum.108 = f32[32,256]{1,0:T(8,128)S(1)} all-reduce(f32[32,256]{1,0:T(8,128)S(1)} %fusion.96), channel_id=1, replica_groups=mesh['layer'=2,'row'=4,'col'=4] {'col'}, use_global_device_ids=true, to_apply=%region_1.1 | all-reduce | flops 8192 | bytes 65536 | tf_op jit(solution)/shard_map/while/body/eval_jaxpr/psum | solution.py:28
  126.5 15.8 %psum.108 = f32[32,256]{1,0:T(8,128)S(1)} all-reduce(f32[32,256]{1,0:T(8,128)S(1)} %fusion.96), channel_id=1, replica_groups=mesh['layer'=2,'row'=4,'col'=4] {'col'}, use_global_device_ids=true, to_apply=%region_1.1 | all-reduce | flops 8192 | bytes 65536 | tf_op jit(solution)/shard_map/while/body/eval_jaxpr/psum | solution.py:28
  161.3 17.5 %psum.108 = f32[32,256]{1,0:T(8,128)S(1)} all-reduce(f32[32,256]{1,0:T(8,128)S(1)} %fusion.96), channel_id=1, replica_groups=mesh['layer'=2,'row'=4,'col'=4] {'col'}, use_global_device_ids=true, to_apply=%region_1.1 | all-reduce | flops 8192 | bytes 65536 | tf_op jit(solution)/shard_map/while/body/eval_jaxpr/psum | solution.py:28
  180.1 16.3 %psum.109 = f32[1,32,256]{2,1,0:T(8,128)S(1)} all-reduce(f32[1,32,256]{2,1,0:T(8,128)S(1)} %convolution_bitcast_fusion.8), channel_id=1, replica_groups=mesh['layer'=2,'row'=4,'col'=4] {'row'}, use_global_device_ids=true, to_apply=%region_2.2 | all-reduce | flops 8192 | bytes 65536 | tf_op jit(solution)/shard_map/while/body/eval_jaxpr/psum | solution.py:30
  199.9 15.8 %psum.108 = f32[32,256]{1,0:T(8,128)S(1)} all-reduce(f32[32,256]{1,0:T(8,128)S(1)} %fusion.96), channel_id=1, replica_groups=mesh['layer'=2,'row'=4,'col'=4] {'col'}, use_global_device_ids=true, to_apply=%region_1.1 | all-reduce | flops 8192 | bytes 65536 | tf_op jit(solution)/shard_map/while/body/eval_jaxpr/psum | solution.py:28
  234.8 17.4 %psum.108 = f32[32,256]{1,0:T(8,128)S(1)} all-reduce(f32[32,256]{1,0:T(8,128)S(1)} %fusion.96), channel_id=1, replica_groups=mesh['layer'=2,'row'=4,'col'=4] {'col'}, use_global_device_ids=true, to_apply=%region_1.1 | all-reduce | flops 8192 | bytes 65536 | tf_op jit(solution)/shard_map/while/body/eval_jaxpr/psum | solution.py:28
  272.6 15.8 %psum.108 = f32[32,256]{1,0:T(8,128)S(1)} all-reduce(f32[32,256]{1,0:T(8,128)S(1)} %fusion.96), channel_id=1, replica_groups=mesh['layer'=2,'row'=4,'col'=4] {'col'}, use_global_device_ids=true, to_apply=%region_1.1 | all-reduce | flops 8192 | bytes 65536 | tf_op jit(solution)/shard_map/while/body/eval_jaxpr/psum | solution.py:28
  303.9 19.2 %fusion.56 = f32[8,32,256]{2,1,0:T(8,128)} fusion(f32[1,8,8,256,256]{4,3,2,1,0:T(8,128)} %param.19, f32[8,32,256]{2,1,0:T(8,128)S(1)} %get-tuple-element.861), kind=kOutput, calls=%fused_computation.48 | convolution fusion | flops 1610612736 | bytes 17301504 | tf_op jit(solution)/shard_map/jna,kjba->knb/dot_general | solution.py:74
  330.4 284.1 %while.57 = (s32[]{:T(128)}, f32[8,16,256]{2,1,0:T(8,128)S(1)}, pred[]{:T(512)}, f32[8,16,256]{2,1,0:T(8,128)S(1)}, f32[8,16,256]{2,1,0:T(8,128)}, /*index=5*/f3...) while((s32[]{:T(128)}, f32[8,16,256]{2,1,0:T(8,128)S(1)}, pred[]{:T(512)}, ...), condition=%wide.region_8.9_spmd, body=%wide.region_5.8_spmd.sunk | while | flops 113266688 | bytes 2672229 | solution.py:33
  333.7 18.9 %psum.110 = f32[16,256]{1,0:T(8,128)S(1)} all-reduce(f32[16,256]{1,0:T(8,128)S(1)} %fusion.101), channel_id=1, replica_groups=mesh['layer'=2,'row'=4,'col'=4] {'col'}, use_global_device_ids=true, to_apply=%region_6.6 | all-reduce | flops 4096 | bytes 32768 | tf_op jit(solution)/shard_map/while/body/eval_jaxpr/psum | solution.py:28
  353.9 16.1 %psum.111 = f32[1,16,256]{2,1,0:T(8,128)S(1)} all-reduce(f32[1,16,256]{2,1,0:T(8,128)S(1)} %convolution_bitcast_fusion.9), channel_id=1, replica_groups=mesh['layer'=2,'row'=4,'col'=4] {'row'}, use_global_device_ids=true, to_apply=%region_7.7 | all-reduce | flops 4096 | bytes 32768 | tf_op jit(solution)/shard_map/while/body/eval_jaxpr/psum | solution.py:30
  407.2 16.3 %psum.110 = f32[16,256]{1,0:T(8,128)S(1)} all-reduce(f32[16,256]{1,0:T(8,128)S(1)} %fusion.101), channel_id=1, replica_groups=mesh['layer'=2,'row'=4,'col'=4] {'col'}, use_global_device_ids=true, to_apply=%region_6.6 | all-reduce | flops 4096 | bytes 32768 | tf_op jit(solution)/shard_map/while/body/eval_jaxpr/psum | solution.py:28
  477.4 16.3 %psum.110 = f32[16,256]{1,0:T(8,128)S(1)} all-reduce(f32[16,256]{1,0:T(8,128)S(1)} %fusion.101), channel_id=1, replica_groups=mesh['layer'=2,'row'=4,'col'=4] {'col'}, use_global_device_ids=true, to_apply=%region_6.6 | all-reduce | flops 4096 | bytes 32768 | tf_op jit(solution)/shard_map/while/body/eval_jaxpr/psum | solution.py:28
  547.6 16.3 %psum.110 = f32[16,256]{1,0:T(8,128)S(1)} all-reduce(f32[16,256]{1,0:T(8,128)S(1)} %fusion.101), channel_id=1, replica_groups=mesh['layer'=2,'row'=4,'col'=4] {'col'}, use_global_device_ids=true, to_apply=%region_6.6 | all-reduce | flops 4096 | bytes 32768 | tf_op jit(solution)/shard_map/while/body/eval_jaxpr/psum | solution.py:28
  614.5 274.9 %while.58 = (s32[]{:T(128)}, f32[8,16,256]{2,1,0:T(8,128)S(1)}, pred[]{:T(512)}, f32[8,16,256]{2,1,0:T(8,128)S(1)}, f32[8,8,256,256]{3,2,1,0:T(8,128)}, /*index=...) while((s32[]{:T(128)}, f32[8,16,256]{2,1,0:T(8,128)S(1)}, pred[]{:T(512)}, ...), condition=%wide.region_12.13_spmd, body=%wide.region_9.12_spmd.sunk | while | flops 113262600 | bytes 2655907 | solution.py:56
  633.8 16.3 %psum.113 = f32[1,16,256]{2,1,0:T(8,128)S(1)} all-reduce(f32[1,16,256]{2,1,0:T(8,128)S(1)} %convolution_bitcast_fusion.10), channel_id=1, replica_groups=mesh['layer'=2,'row'=4,'col'=4] {'col'}, use_global_device_ids=true, to_apply=%region_11.11 | all-reduce | flops 4096 | bytes 32768 | tf_op jit(solution)/shard_map/while/body/eval_jaxpr/psum | solution.py:53
  702.5 16.2 %psum.113 = f32[1,16,256]{2,1,0:T(8,128)S(1)} all-reduce(f32[1,16,256]{2,1,0:T(8,128)S(1)} %convolution_bitcast_fusion.10), channel_id=1, replica_groups=mesh['layer'=2,'row'=4,'col'=4] {'col'}, use_global_device_ids=true, to_apply=%region_11.11 | all-reduce | flops 4096 | bytes 32768 | tf_op jit(solution)/shard_map/while/body/eval_jaxpr/psum | solution.py:53
  771.2 16.3 %psum.113 = f32[1,16,256]{2,1,0:T(8,128)S(1)} all-reduce(f32[1,16,256]{2,1,0:T(8,128)S(1)} %convolution_bitcast_fusion.10), channel_id=1, replica_groups=mesh['layer'=2,'row'=4,'col'=4] {'col'}, use_global_device_ids=true, to_apply=%region_11.11 | all-reduce | flops 4096 | bytes 32768 | tf_op jit(solution)/shard_map/while/body/eval_jaxpr/psum | solution.py:53
  839.9 16.3 %psum.113 = f32[1,16,256]{2,1,0:T(8,128)S(1)} all-reduce(f32[1,16,256]{2,1,0:T(8,128)S(1)} %convolution_bitcast_fusion.10), channel_id=1, replica_groups=mesh['layer'=2,'row'=4,'col'=4] {'col'}, use_global_device_ids=true, to_apply=%region_11.11 | all-reduce | flops 4096 | bytes 32768 | tf_op jit(solution)/shard_map/while/body/eval_jaxpr/psum | solution.py:53
  905.6 285.7 %while.59 = (s32[]{:T(128)}, f32[8,32,256]{2,1,0:T(8,128)S(1)}, pred[]{:T(512)}, f32[8,32,256]{2,1,0:T(8,128)S(1)}, f32[8,32,256]{2,1,0:T(8,128)S(1)}, /*index=5...) while((s32[]{:T(128)}, f32[8,32,256]{2,1,0:T(8,128)S(1)}, ...), condition=%wide.region_16.17_spmd, body=%wide.region_13.16_spmd.sunk | while | flops 226533376 | bytes 2983595 | solution.py:56
  925.2 16.6 %psum.115 = f32[1,32,256]{2,1,0:T(8,128)S(1)} all-reduce(f32[1,32,256]{2,1,0:T(8,128)S(1)} %convolution_bitcast_fusion.11), channel_id=1, replica_groups=mesh['layer'=2,'row'=4,'col'=4] {'col'}, use_global_device_ids=true, to_apply=%region_15.15 | all-reduce | flops 8192 | bytes 65536 | tf_op jit(solution)/shard_map/while/body/eval_jaxpr/psum | solution.py:53
  960.0 16.7 %psum.115 = f32[1,32,256]{2,1,0:T(8,128)S(1)} all-reduce(f32[1,32,256]{2,1,0:T(8,128)S(1)} %convolution_bitcast_fusion.11), channel_id=1, replica_groups=mesh['layer'=2,'row'=4,'col'=4] {'col'}, use_global_device_ids=true, to_apply=%region_15.15 | all-reduce | flops 8192 | bytes 65536 | tf_op jit(solution)/shard_map/while/body/eval_jaxpr/psum | solution.py:53
  996.2 16.6 %psum.115 = f32[1,32,256]{2,1,0:T(8,128)S(1)} all-reduce(f32[1,32,256]{2,1,0:T(8,128)S(1)} %convolution_bitcast_fusion.11), channel_id=1, replica_groups=mesh['layer'=2,'row'=4,'col'=4] {'col'}, use_global_device_ids=true, to_apply=%region_15.15 | all-reduce | flops 8192 | bytes 65536 | tf_op jit(solution)/shard_map/while/body/eval_jaxpr/psum | solution.py:53
  1031.6 16.9 %psum.115 = f32[1,32,256]{2,1,0:T(8,128)S(1)} all-reduce(f32[1,32,256]{2,1,0:T(8,128)S(1)} %convolution_bitcast_fusion.11), channel_id=1, replica_groups=mesh['layer'=2,'row'=4,'col'=4] {'col'}, use_global_device_ids=true, to_apply=%region_15.15 | all-reduce | flops 8192 | bytes 65536 | tf_op jit(solution)/shard_map/while/body/eval_jaxpr/psum | solution.py:53
  1068.0 16.7 %psum.115 = f32[1,32,256]{2,1,0:T(8,128)S(1)} all-reduce(f32[1,32,256]{2,1,0:T(8,128)S(1)} %convolution_bitcast_fusion.11), channel_id=1, replica_groups=mesh['layer'=2,'row'=4,'col'=4] {'col'}, use_global_device_ids=true, to_apply=%region_15.15 | all-reduce | flops 8192 | bytes 65536 | tf_op jit(solution)/shard_map/while/body/eval_jaxpr/psum | solution.py:53
  1103.0 16.7 %psum.115 = f32[1,32,256]{2,1,0:T(8,128)S(1)} all-reduce(f32[1,32,256]{2,1,0:T(8,128)S(1)} %convolution_bitcast_fusion.11), channel_id=1, replica_groups=mesh['layer'=2,'row'=4,'col'=4] {'col'}, use_global_device_ids=true, to_apply=%region_15.15 | all-reduce | flops 8192 | bytes 65536 | tf_op jit(solution)/shard_map/while/body/eval_jaxpr/psum | solution.py:53
  1139.1 16.6 %psum.115 = f32[1,32,256]{2,1,0:T(8,128)S(1)} all-reduce(f32[1,32,256]{2,1,0:T(8,128)S(1)} %convolution_bitcast_fusion.11), channel_id=1, replica_groups=mesh['layer'=2,'row'=4,'col'=4] {'col'}, use_global_device_ids=true, to_apply=%region_15.15 | all-reduce | flops 8192 | bytes 65536 | tf_op jit(solution)/shard_map/while/body/eval_jaxpr/psum | solution.py:53
  1174.3 16.9 %psum.115 = f32[1,32,256]{2,1,0:T(8,128)S(1)} all-reduce(f32[1,32,256]{2,1,0:T(8,128)S(1)} %convolution_bitcast_fusion.11), channel_id=1, replica_groups=mesh['layer'=2,'row'=4,'col'=4] {'col'}, use_global_device_ids=true, to_apply=%region_15.15 | all-reduce | flops 8192 | bytes 65536 | tf_op jit(solution)/shard_map/while/body/eval_jaxpr/psum | solution.py:53
  (149 shorter events, 712.7 us)
Async XLA Ops:
  7.2 316.0 %copy-start = (f32[32,8,256]{2,1,0:T(8,128)S(1)}, f32[32,8,256]{2,1,0:T(8,128)}, u32[]{:S(2)}) copy-start(f32[32,8,256]{2,1,0:T(8,128)} %param.15) | copy-start | bytes 786436
  7.2 323.2 %reduce-scatter.2.cloned.1.call-start = ((), (), s32[]{:S(2)}) async-start(), calls=%async_computation.1 | async-start | bytes 393216 | tf_op jit(solution)/shard_map/reduce_scatter | solution.py:75
Sparse Core Ops, SparseCore 0:
  323.2 7.0 reduce-scatter.1
where the time goes:
time: 1200 us
  blocking collectives  1000 us (83%)
  matrix products  169 us (14%)
  between operations  14.1 us (1%)
    psum x16, blocking collectives, forward_step(): residual = lax.psum(partial_value, 'col')  266 us
    psum x16, blocking collectives, backward_step(): solved_block = lax.psum(share, 'col')  261 us
    psum x16, blocking collectives, forward_step(): solved_block = lax.psum(share, 'row')  238 us
    psum x16, blocking collectives, backward_step(): pending = lax.psum(partial_value, 'row')  236 us
    dot_general x16, matrix products, forward_step(): jnp.einsum('jna,jba->nb', solved, row_tiles, precision=precise)  54.5 us
    dot_general x16, matrix products, backward_step(): jnp.einsum('inb,iba->na', solved, column_tiles, precision=precise)  43.7 us
  transfers between devices with their start and end apart: 1, of which 1 were waited for; matrix products, arithmetic and copies ran while one was open for 0% of the time, Pallas kernels for 0%

commit v1 on v0

--- a/solution.py
+++ b/solution.py
@@ -50,7 +50,8 @@
         )
         pending = lax.psum(partial_value, "row")
         share = jnp.einsum("na,ab->nb", pending, pick(inverse, target, 0), precision=precise)
-        solved_block = lax.psum(share, "col")
+        shards = lax.all_gather(share, "col", axis=0, tiled=False)
+        solved_block = shards.sum(axis=0)
         return lax.dynamic_update_index_in_dim(solved, solved_block, target, 0)
 
     return lax.fori_loop(0, blocks, backward_step, solved)

time: 1200 us -> 1150 us (0.958)
  blocking collectives: 1000 us -> 955 us
    psum x16 -> x0, blocking collectives: 261 us -> none  [backward_step(): solved_block = lax.psum(share, 'col')]
    all_gather x0 -> x16, blocking collectives: none -> 212 us  [backward_step(): shards = lax.all_gather(share, 'col', axis=0, tiled=False)]
where the time goes in v1:
time: 1150 us
  blocking collectives  955 us (83%)
  matrix products  169 us (15%)
  between operations  14.1 us (1%)
    psum x16, blocking collectives, forward_step(): residual = lax.psum(partial_value, 'col')  266 us
    psum x16, blocking collectives, forward_step(): solved_block = lax.psum(share, 'row')  238 us
    psum x16, blocking collectives, backward_step(): pending = lax.psum(partial_value, 'row')  237 us
    all_gather x16, blocking collectives, backward_step(): shards = lax.all_gather(share, 'col', axis=0, tiled=False)  212 us
    dot_general x16, matrix products, forward_step(): jnp.einsum('jna,jba->nb', solved, row_tiles, precision=precise)  54.5 us
    dot_general x16, matrix products, backward_step(): jnp.einsum('inb,iba->na', solved, column_tiles, precision=precise)  43.8 us
  transfers between devices with their start and end apart: 1, of which 1 were waited for; matrix products, arithmetic and copies ran while one was open for 0% of the time, Pallas kernels for 0%

profile of v1, /device:TPU:0, one launch (start us, length us, event | category | flops | bytes accessed | tf_op | source)
XLA Modules:
  0.0 1150.8 jit_solution(12990924160389497837)
XLA Ops:
  8.3 295.6 %while.56 = (s32[]{:T(128)}, f32[8,32,256]{2,1,0:T(8,128)S(1)}, pred[]{:T(512)}, f32[8,32,256]{2,1,0:T(8,128)S(1)}, f32[8,8,256,256]{3,2,1,0:T(8,128)}, /*index=5*/f32[8,256,256]{2,1,0:T(8,128)}, s32[]{:T(128)}) while((s32[]{:T(128)}, f32[8,32,256]{2,1,0:T(8,128)S(1)}, pred[]{:T(512)}, f32[8,32,256]{2,1,0:T(8,128)S(1)}, ...), condition=%wide.region_3.4_spmd, body=%wide.region_0.3_spmd.sunk | while | flops 226525184 | bytes 2950749 | solution.py:33
  11.8 20.9 %psum.78 = f32[32,256]{1,0:T(8,128)S(1)} all-reduce(f32[32,256]{1,0:T(8,128)S(1)} %fusion.100), channel_id=1, replica_groups=mesh['layer'=2,'row'=4,'col'=4] {'col'}, use_global_device_ids=true, to_apply=%region_1.1 | all-reduce | flops 8192 | bytes 65536 | tf_op jit(solution)/shard_map/while/body/eval_jaxpr/psum | solution.py:28
  34.0 16.3 %psum.79 = f32[1,32,256]{2,1,0:T(8,128)S(1)} all-reduce(f32[1,32,256]{2,1,0:T(8,128)S(1)} %convolution_bitcast_fusion.4), channel_id=1, replica_groups=mesh['layer'=2,'row'=4,'col'=4] {'row'}, use_global_device_ids=true, to_apply=%region_2.2 | all-reduce | flops 8192 | bytes 65536 | tf_op jit(solution)/shard_map/while/body/eval_jaxpr/psum | solution.py:30
  53.8 15.8 %psum.78 = f32[32,256]{1,0:T(8,128)S(1)} all-reduce(f32[32,256]{1,0:T(8,128)S(1)} %fusion.100), channel_id=1, replica_groups=mesh['layer'=2,'row'=4,'col'=4] {'col'}, use_global_device_ids=true, to_apply=%region_1.1 | all-reduce | flops 8192 | bytes 65536 | tf_op jit(solution)/shard_map/while/body/eval_jaxpr/psum | solution.py:28
  88.6 17.5 %psum.78 = f32[32,256]{1,0:T(8,128)S(1)} all-reduce(f32[32,256]{1,0:T(8,128)S(1)} %fusion.100), channel_id=1, replica_groups=mesh['layer'=2,'row'=4,'col'=4] {'col'}, use_global_device_ids=true, to_apply=%region_1.1 | all-reduce | flops 8192 | bytes 65536 | tf_op jit(solution)/shard_map/while/body/eval_jaxpr/psum | solution.py:28
  107.5 15.6 %psum.79 = f32[1,32,256]{2,1,0:T(8,128)S(1)} all-reduce(f32[1,32,256]{2,1,0:T(8,128)S(1)} %convolution_bitcast_fusion.4), channel_id=1, replica_groups=mesh['layer'=2,'row'=4,'col'=4] {'row'}, use_global_device_ids=true, to_apply=%region_2.2 | all-reduce | flops 8192 | bytes 65536 | tf_op jit(solution)/shard_map/while/body/eval_jaxpr/psum | solution.py:30
  126.5 15.8 %psum.78 = f32[32,256]{1,0:T(8,128)S(1)} all-reduce(f32[32,256]{1,0:T(8,128)S(1)} %fusion.100), channel_id=1, replica_groups=mesh['layer'=2,'row'=4,'col'=4] {'col'}, use_global_device_ids=true, to_apply=%region_1.1 | all-reduce | flops 8192 | bytes 65536 | tf_op jit(solution)/shard_map/while/body/eval_jaxpr/psum | solution.py:28
  161.3 17.5 %psum.78 = f32[32,256]{1,0:T(8,128)S(1)} all-reduce(f32[32,256]{1,0:T(8,128)S(1)} %fusion.100), channel_id=1, replica_groups=mesh['layer'=2,'row'=4,'col'=4] {'col'}, use_global_device_ids=true, to_apply=%region_1.1 | all-reduce | flops 8192 | bytes 65536 | tf_op jit(solution)/shard_map/while/body/eval_jaxpr/psum | solution.py:28
  180.1 16.3 %psum.79 = f32[1,32,256]{2,1,0:T(8,128)S(1)} all-reduce(f32[1,32,256]{2,1,0:T(8,128)S(1)} %convolution_bitcast_fusion.4), channel_id=1, replica_groups=mesh['layer'=2,'row'=4,'col'=4] {'row'}, use_global_device_ids=true, to_apply=%region_2.2 | all-reduce | flops 8192 | bytes 65536 | tf_op jit(solution)/shard_map/while/body/eval_jaxpr/psum | solution.py:30
  199.9 15.8 %psum.78 = f32[32,256]{1,0:T(8,128)S(1)} all-reduce(f32[32,256]{1,0:T(8,128)S(1)} %fusion.100), channel_id=1, replica_groups=mesh['layer'=2,'row'=4,'col'=4] {'col'}, use_global_device_ids=true, to_apply=%region_1.1 | all-reduce | flops 8192 | bytes 65536 | tf_op jit(solution)/shard_map/while/body/eval_jaxpr/psum | solution.py:28
  234.8 17.4 %psum.78 = f32[32,256]{1,0:T(8,128)S(1)} all-reduce(f32[32,256]{1,0:T(8,128)S(1)} %fusion.100), channel_id=1, replica_groups=mesh['layer'=2,'row'=4,'col'=4] {'col'}, use_global_device_ids=true, to_apply=%region_1.1 | all-reduce | flops 8192 | bytes 65536 | tf_op jit(solution)/shard_map/while/body/eval_jaxpr/psum | solution.py:28
  253.5 15.6 %psum.79 = f32[1,32,256]{2,1,0:T(8,128)S(1)} all-reduce(f32[1,32,256]{2,1,0:T(8,128)S(1)} %convolution_bitcast_fusion.4), channel_id=1, replica_groups=mesh['layer'=2,'row'=4,'col'=4] {'row'}, use_global_device_ids=true, to_apply=%region_2.2 | all-reduce | flops 8192 | bytes 65536 | tf_op jit(solution)/shard_map/while/body/eval_jaxpr/psum | solution.py:30
  272.6 15.8 %psum.78 = f32[32,256]{1,0:T(8,128)S(1)} all-reduce(f32[32,256]{1,0:T(8,128)S(1)} %fusion.100), channel_id=1, replica_groups=mesh['layer'=2,'row'=4,'col'=4] {'col'}, use_global_device_ids=true, to_apply=%region_1.1 | all-reduce | flops 8192 | bytes 65536 | tf_op jit(solution)/shard_map/while/body/eval_jaxpr/psum | solution.py:28
  303.9 19.2 %fusion.58 = f32[8,32,256]{2,1,0:T(8,128)} fusion(f32[1,8,8,256,256]{4,3,2,1,0:T(8,128)} %param.19, f32[8,32,256]{2,1,0:T(8,128)S(1)} %get-tuple-element.864), kind=kOutput, calls=%fused_computation.48 | convolution fusion | flops 1610612736 | bytes 17301504 | tf_op jit(solution)/shard_map/jna,kjba->knb/dot_general | solution.py:75
  330.4 284.1 %while.57 = (s32[]{:T(128)}, f32[8,16,256]{2,1,0:T(8,128)S(1)}, pred[]{:T(512)}, f32[8,16,256]{2,1,0:T(8,128)S(1)}, f32[8,16,256]{2,1,0:T(8,128)}, /*index=5*/f3...) while((s32[]{:T(128)}, f32[8,16,256]{2,1,0:T(8,128)S(1)}, pred[]{:T(512)}, ...), condition=%wide.region_8.9_spmd, body=%wide.region_5.8_spmd.sunk | while | flops 113266688 | bytes 2672229 | solution.py:33
  333.7 18.9 %psum.80 = f32[16,256]{1,0:T(8,128)S(1)} all-reduce(f32[16,256]{1,0:T(8,128)S(1)} %fusion.105), channel_id=1, replica_groups=mesh['layer'=2,'row'=4,'col'=4] {'col'}, use_global_device_ids=true, to_apply=%region_6.6 | all-reduce | flops 4096 | bytes 32768 | tf_op jit(solution)/shard_map/while/body/eval_jaxpr/psum | solution.py:28
  353.9 16.1 %psum.81 = f32[1,16,256]{2,1,0:T(8,128)S(1)} all-reduce(f32[1,16,256]{2,1,0:T(8,128)S(1)} %convolution_bitcast_fusion.5), channel_id=1, replica_groups=mesh['layer'=2,'row'=4,'col'=4] {'row'}, use_global_device_ids=true, to_apply=%region_7.7 | all-reduce | flops 4096 | bytes 32768 | tf_op jit(solution)/shard_map/while/body/eval_jaxpr/psum | solution.py:30
  373.3 15.6 %psum.80 = f32[16,256]{1,0:T(8,128)S(1)} all-reduce(f32[16,256]{1,0:T(8,128)S(1)} %fusion.105), channel_id=1, replica_groups=mesh['layer'=2,'row'=4,'col'=4] {'col'}, use_global_device_ids=true, to_apply=%region_6.6 | all-reduce | flops 4096 | bytes 32768 | tf_op jit(solution)/shard_map/while/body/eval_jaxpr/psum | solution.py:28
  407.2 16.3 %psum.80 = f32[16,256]{1,0:T(8,128)S(1)} all-reduce(f32[16,256]{1,0:T(8,128)S(1)} %fusion.105), channel_id=1, replica_groups=mesh['layer'=2,'row'=4,'col'=4] {'col'}, use_global_device_ids=true, to_apply=%region_6.6 | all-reduce | flops 4096 | bytes 32768 | tf_op jit(solution)/shard_map/while/body/eval_jaxpr/psum | solution.py:28
  424.7 15.4 %psum.81 = f32[1,16,256]{2,1,0:T(8,128)S(1)} all-reduce(f32[1,16,256]{2,1,0:T(8,128)S(1)} %convolution_bitcast_fusion.5), channel_id=1, replica_groups=mesh['layer'=2,'row'=4,'col'=4] {'row'}, use_global_device_ids=true, to_apply=%region_7.7 | all-reduce | flops 4096 | bytes 32768 | tf_op jit(solution)/shard_map/while/body/eval_jaxpr/psum | solution.py:30
  443.5 15.6 %psum.80 = f32[16,256]{1,0:T(8,128)S(1)} all-reduce(f32[16,256]{1,0:T(8,128)S(1)} %fusion.105), channel_id=1, replica_groups=mesh['layer'=2,'row'=4,'col'=4] {'col'}, use_global_device_ids=true, to_apply=%region_6.6 | all-reduce | flops 4096 | bytes 32768 | tf_op jit(solution)/shard_map/while/body/eval_jaxpr/psum | solution.py:28
  477.4 16.3 %psum.80 = f32[16,256]{1,0:T(8,128)S(1)} all-reduce(f32[16,256]{1,0:T(8,128)S(1)} %fusion.105), channel_id=1, replica_groups=mesh['layer'=2,'row'=4,'col'=4] {'col'}, use_global_device_ids=true, to_apply=%region_6.6 | all-reduce | flops 4096 | bytes 32768 | tf_op jit(solution)/shard_map/while/body/eval_jaxpr/psum | solution.py:28
  513.7 15.6 %psum.80 = f32[16,256]{1,0:T(8,128)S(1)} all-reduce(f32[16,256]{1,0:T(8,128)S(1)} %fusion.105), channel_id=1, replica_groups=mesh['layer'=2,'row'=4,'col'=4] {'col'}, use_global_device_ids=true, to_apply=%region_6.6 | all-reduce | flops 4096 | bytes 32768 | tf_op jit(solution)/shard_map/while/body/eval_jaxpr/psum | solution.py:28
  547.6 16.3 %psum.80 = f32[16,256]{1,0:T(8,128)S(1)} all-reduce(f32[16,256]{1,0:T(8,128)S(1)} %fusion.105), channel_id=1, replica_groups=mesh['layer'=2,'row'=4,'col'=4] {'col'}, use_global_device_ids=true, to_apply=%region_6.6 | all-reduce | flops 4096 | bytes 32768 | tf_op jit(solution)/shard_map/while/body/eval_jaxpr/psum | solution.py:28
  583.9 15.6 %psum.80 = f32[16,256]{1,0:T(8,128)S(1)} all-reduce(f32[16,256]{1,0:T(8,128)S(1)} %fusion.105), channel_id=1, replica_groups=mesh['layer'=2,'row'=4,'col'=4] {'col'}, use_global_device_ids=true, to_apply=%region_6.6 | all-reduce | flops 4096 | bytes 32768 | tf_op jit(solution)/shard_map/while/body/eval_jaxpr/psum | solution.py:28
  614.5 253.1 %while.58 = (s32[]{:T(128)}, f32[8,16,256]{2,1,0:T(8,128)S(1)}, pred[]{:T(512)}, f32[8,16,256]{2,1,0:T(8,128)S(1)}, f32[8,8,256,256]{3,2,1,0:T(8,128)}, /*index=...) while((s32[]{:T(128)}, f32[8,16,256]{2,1,0:T(8,128)S(1)}, ...), condition=%wide.region_12.13_spmd, body=%wide.region_9.12_spmd.sunk | while | flops 113270792 | bytes 2786991 | solution.py:57
  680.4 15.4 %psum.82 = f32[16,256]{1,0:T(8,128)S(1)} all-reduce(f32[16,256]{1,0:T(8,128)S(1)} %fusion.110), channel_id=1, replica_groups=mesh['layer'=2,'row'=4,'col'=4] {'row'}, use_global_device_ids=true, to_apply=%region_10.10 | all-reduce | flops 4096 | bytes 32768 | tf_op jit(solution)/shard_map/while/body/eval_jaxpr/psum | solution.py:51
  883.8 259.3 %while.59 = (s32[]{:T(128)}, f32[8,32,256]{2,1,0:T(8,128)S(1)}, pred[]{:T(512)}, f32[8,32,256]{2,1,0:T(8,128)S(1)}, f32[8,32,256]{2,1,0:T(8,128)S(1)}, /*index=5...) while((s32[]{:T(128)}, f32[8,32,256]{2,1,0:T(8,128)S(1)}, ...), condition=%wide.region_16.17_spmd, body=%wide.region_13.16_spmd.sunk | while | flops 226549760 | bytes 3245751 | solution.py:57
  886.6 15.6 %psum.83 = f32[32,256]{1,0:T(8,128)S(1)} all-reduce(f32[32,256]{1,0:T(8,128)S(1)} %fusion.116), channel_id=1, replica_groups=mesh['layer'=2,'row'=4,'col'=4] {'row'}, use_global_device_ids=true, to_apply=%region_14.14 | all-reduce | flops 8192 | bytes 65536 | tf_op jit(solution)/shard_map/while/body/eval_jaxpr/psum | solution.py:51
  951.1 15.6 %psum.83 = f32[32,256]{1,0:T(8,128)S(1)} all-reduce(f32[32,256]{1,0:T(8,128)S(1)} %fusion.116), channel_id=1, replica_groups=mesh['layer'=2,'row'=4,'col'=4] {'row'}, use_global_device_ids=true, to_apply=%region_14.14 | all-reduce | flops 8192 | bytes 65536 | tf_op jit(solution)/shard_map/while/body/eval_jaxpr/psum | solution.py:51
  1016.3 15.8 %psum.83 = f32[32,256]{1,0:T(8,128)S(1)} all-reduce(f32[32,256]{1,0:T(8,128)S(1)} %fusion.116), channel_id=1, replica_groups=mesh['layer'=2,'row'=4,'col'=4] {'row'}, use_global_device_ids=true, to_apply=%region_14.14 | all-reduce | flops 8192 | bytes 65536 | tf_op jit(solution)/shard_map/while/body/eval_jaxpr/psum | solution.py:51
  1080.8 15.7 %psum.83 = f32[32,256]{1,0:T(8,128)S(1)} all-reduce(f32[32,256]{1,0:T(8,128)S(1)} %fusion.116), channel_id=1, replica_groups=mesh['layer'=2,'row'=4,'col'=4] {'row'}, use_global_device_ids=true, to_apply=%region_14.14 | all-reduce | flops 8192 | bytes 65536 | tf_op jit(solution)/shard_map/while/body/eval_jaxpr/psum | solution.py:51
  (165 shorter events, 676.1 us)
Async XLA Ops:
  7.2 316.0 %copy-start = (f32[32,8,256]{2,1,0:T(8,128)S(1)}, f32[32,8,256]{2,1,0:T(8,128)}, u32[]{:S(2)}) copy-start(f32[32,8,256]{2,1,0:T(8,128)} %param.15) | copy-start | bytes 786436
  7.2 323.2 %reduce-scatter.2.cloned.1.call-start = ((), (), s32[]{:S(2)}) async-start(), calls=%async_computation.1 | async-start | bytes 393216 | tf_op jit(solution)/shard_map/reduce_scatter | solution.py:76
Sparse Core Ops, SparseCore 0:
  323.2 7.0 reduce-scatter.1
